TPU v7x, 32 devices: a whole 2x2x4 slice. The times are simulated.
32 devices in a mesh: rep: 16 (over z, y, core), tp: 2 (over x).
Axes of the slice: x: 2, y: 2, z: 4, core: 2. Of those that a mesh axis runs over, the one named last changes fastest.
Arguments:
- activations: bfloat16 [8192, 6144], P('rep', 'tp'), may hold values from -6 to 6
- norm_gain: float32 [6144], replicated, may hold values from 0.5 to 1.5
- query_gain: float32 [128], replicated, may hold values from 0.5 to 18
- key_gain: float32 [128], replicated, may hold values from 0.5 to 18
- project_in: bfloat16 [6144, 24, 384], P('rep', 'tp'), may hold values from -1 to 1
- project_out: bfloat16 [6144, 3072], P('rep', 'tp'), may hold values from -1 to 1
Outputs:
- attended: bfloat16 [8192, 6144], P('rep', 'tp')
- weight_norms: float32 [2], replicated
All inputs are finite; a program needn't handle non-finite values.
Results may differ from a plain program's by a relative error of at most 0.018.
The roundings to bfloat16 on the way count: a program that leaves them out, or rounds other values in their place, can miss the bound.
Values may be sent and summed in bfloat16 or wider, within the bound.
A program may use at most 192 MiB of HBM per device.

v0:
```python
import functools
import math
import jax
import jax.numpy as jnp
from jax import lax
from jax.sharding import PartitionSpec as P

D = 6144
HEADS = 24
HEAD_DIM = 128
PATCHES = 256


def layer_norm(values, gain):
    average = jnp.mean(values, -1, keepdims=True)
    centred = values - average
    variance = jnp.mean(centred * centred, -1, keepdims=True)
    return centred * lax.rsqrt(variance + 1e-06) * gain


def heads_mixed(projected, query_gain, key_gain, head_dim):
    tok_rows, width = projected.shape
    heads = width // (3 * head_dim)
    projected = projected.reshape(tok_rows // PATCHES, PATCHES, heads, 3 * head_dim)
    queries = layer_norm(projected[..., :head_dim], query_gain).astype(jnp.bfloat16)
    keys_normed = layer_norm(projected[..., head_dim : 2 * head_dim], key_gain).astype(jnp.bfloat16)
    values = projected[..., 2 * head_dim :].astype(jnp.bfloat16)
    scores = jnp.einsum(
        "iphd,iqhd->ihpq", queries, keys_normed, preferred_element_type=jnp.float32
    ) / math.sqrt(head_dim)
    probabilities = jax.nn.softmax(scores, axis=-1).astype(jnp.bfloat16)
    mixed = jnp.einsum("ihpq,iqhd->iphd", probabilities, values, preferred_element_type=jnp.float32)
    return mixed.astype(jnp.bfloat16).reshape(tok_rows, heads * head_dim)


def chunk_count(size, wanted):
    while size % wanted:
        wanted -= 1
    return wanted


def shards(n_rep, n_tp, activations, norm_gain, query_gain, key_gain, project_in, project_out):
    me = lax.axis_index("tp")
    swap = [(0, 1), (1, 0)]
    local_rows, local_heads, head_width = project_in.shape
    head_dim = head_width // 3
    n_in = chunk_count(local_heads, 3)
    step = local_heads // n_in
    pieces = []
    for j in range(n_in):
        part = project_in[:, j * step : (j + 1) * step].reshape(local_rows, step * head_width)
        pieces.append(lax.all_gather(part, "rep", axis=0, tiled=True))
    out_rows, out_depth = project_out.shape
    n_out = chunk_count(out_rows // 128, 3) if out_rows % 128 == 0 else 1
    span = out_rows // n_out
    out_pieces = []
    for j in range(n_out):
        part = project_out[j * span : (j + 1) * span]
        out_pieces.append(lax.all_gather(part, "rep", axis=0, tiled=True))
    local_in = jnp.sum(jnp.square(project_in.astype(jnp.float32)))
    local_out = jnp.sum(jnp.square(project_out.astype(jnp.float32)))
    totals = lax.psum(jnp.stack([local_in, local_out]), ("rep", "tp"))
    if n_tp == 2:
        other = lax.ppermute(activations, "tp", swap)
        other, totals = lax.optimization_barrier((other, totals))
        first = jnp.where(me == 0, activations, other)
        second = jnp.where(me == 0, other, activations)
        gathered_rows = jnp.concatenate([first, second], axis=1)
    else:
        gathered_rows = lax.all_gather(activations, "tp", axis=1, tiled=True)
    normed = layer_norm(gathered_rows.astype(jnp.float32), norm_gain).astype(jnp.bfloat16)
    mixed = []
    for piece in pieces:
        projected = jnp.dot(normed, piece, preferred_element_type=jnp.float32)
        mixed.append(heads_mixed(projected, query_gain, key_gain, head_dim))
    mixed = jnp.concatenate(mixed, axis=1)

    def product(rows):
        total = lax.dot_general(
            mixed, rows, (((1,), (1,)), ((), ())), preferred_element_type=jnp.float32
        )
        return total.astype(jnp.bfloat16)

    sums = []
    for piece in out_pieces:
        if n_tp == 2:
            half = piece.shape[0] // 2
            sent = product(lax.dynamic_slice_in_dim(piece, (1 - me) * half, half, 0))
            arrived = lax.ppermute(sent, "tp", swap)
            kept = product(lax.dynamic_slice_in_dim(piece, me * half, half, 0))
            total = kept.astype(jnp.float32) + arrived.astype(jnp.float32)
            sums.append(total.astype(jnp.bfloat16))
        else:
            sums.append(lax.psum_scatter(product(piece), "tp", scatter_dimension=1, tiled=True))
    owners = n_rep // n_tp
    blocks = [sums[j][:, r * span : (r + 1) * span] for r in range(owners) for j in range(n_out)]
    attended = jnp.concatenate(blocks, axis=1)
    fans = jnp.array([3 * HEADS * HEAD_DIM, D], jnp.float32)
    return (attended, jnp.sqrt(totals / fans))


def solution(mesh):
    in_specs = (P("rep", "tp"), P(), P(), P(), P("rep", "tp", None), P("rep", "tp"))
    out_specs = (P("rep", "tp"), P())
    body = functools.partial(shards, mesh.shape["rep"], mesh.shape["tp"])
    return jax.shard_map(body, mesh=mesh, in_specs=in_specs, out_specs=out_specs, check_vma=False)
```

profile of v0, /device:TPU:0, one launch (start us, length us, event | category | flops | bytes accessed | tf_op | source)
XLA Modules:
  0.0 543.6 jit_solution(12540614699131464713)
XLA Ops:
  26.8 98.2 %psum.7 = f32[2]{0:T(128)S(1)} all-reduce(f32[2]{0:T(128)S(1)} %pad_maximum_fusion.1), channel_id=1, replica_groups=mesh['rep'=16,'tp'=2] {'rep','tp'}, use_global_device_ids=true, to_apply=%region_2.0 | all-reduce | flops 2 | bytes 16 | tf_op jit(solution)/shard_map/psum | solution.py:62
  125.0 3.3 broadcast_select_fusion.1
  129.9 4.1 fusion.5
  134.1 16.9 %fusion.109 = f32[512,1536]{1,0:T(8,128)} fusion(bf16[6144,1536]{0,1:T(8,128)(2,1)} %all-gather.9.cloned.1.call-done, f32[6144]{0:T(1024)S(1)} %copy-done.12, f32[512]{0:T(512)S(1)} %add_rsqrt_fusion.6, f32[512]{0:T(512)S(1)} %broadcast_multiply_fusion.6, bf16[512,3072]{1,0:T(8,128)(2,1)} %copy-done, bf16[512,3072]{1,0:T(8,128)(2,1)S(1)} %get-tuple-element.12), kind=kOutput, calls=%fused_computation.164 | convolution fusion | flops 9688842240 | bytes 28340224 | tf_op jit(solution)/shard_map/dot_general | solution.py:74
  151.0 4.8 reshape.128
  155.8 58.2 %all-gather.11.cloned.1.call-done = bf16[6144,1536]{0,1:T(8,128)(2,1)} async-done(((bf16[384,1536]{0,1:T(8,128)(2,1)}), bf16[6144,1536]{0,1:T(8,128)(2,1)}) %all-gather.11.cloned.1.call-update) | async-done | bytes 18874384 | tf_op jit(solution)/shard_map/all_gather | solution.py:52
  214.0 17.3 %fusion.107 = f32[512,1536]{1,0:T(8,128)} fusion(bf16[6144,1536]{0,1:T(8,128)(2,1)} %all-gather.11.cloned.1.call-done, f32[6144]{0:T(1024)S(1)} %copy-done.12, f32[512]{0:T(512)S(1)} %add_rsqrt_fusion.6, f32[512]{0:T(512)S(1)} %broadcast_multiply_fusion.6, bf16[512,3072]{1,0:T(8,128)(2,1)} %copy-done, bf16[512,3072]{1,0:T(8,128)(2,1)S(1)} %get-tuple-element.12), kind=kOutput, calls=%fused_computation.163 | convolution fusion | flops 9688842240 | bytes 28340224 | tf_op jit(solution)/shard_map/dot_general | solution.py:74
  231.3 4.9 reshape.131
  236.2 6.6 %slice_reduce_fusion.1 = (f32[2,256,4]{2,1,0:T(8,128)}, f32[2,256,4]{2,1,0:T(8,128)}, f32[2,256,4,128]{3,2,1,0:T(4,128)}, f32[2,256,4,128]{3,2,1,0:T(4,128)}, f3...) fusion(f32[2,256,4,384]{3,2,1,0:T(4,128)} %reshape.131, ...), kind=kLoop, calls=%fused_computation.158 | loop fusion | flops 1040384 | bytes 8421376 | tf_op jit(solution)/shard_map/reduce_sum | solution.py:15
  260.1 3.5 fusion.49
  277.4 3.4 fusion.48
  282.9 31.5 %all-gather.7.cloned.1.call-done = bf16[6144,1536]{0,1:T(8,128)(2,1)} async-done(((bf16[384,1536]{0,1:T(8,128)(2,1)}), bf16[6144,1536]{0,1:T(8,128)(2,1)}) %all-gather.7.cloned.1.call-update) | async-done | bytes 18874384 | tf_op jit(solution)/shard_map/all_gather | solution.py:52
  314.4 16.6 %fusion.111 = f32[512,1536]{1,0:T(8,128)} fusion(bf16[6144,1536]{0,1:T(8,128)(2,1)} %all-gather.7.cloned.1.call-done, f32[6144]{0:T(1024)S(1)} %copy-done.12, f32[512]{0:T(512)S(1)} %add_rsqrt_fusion.6, f32[512]{0:T(512)S(1)} %broadcast_multiply_fusion.6, bf16[512,3072]{1,0:T(8,128)(2,1)} %copy-done, bf16[512,3072]{1,0:T(8,128)(2,1)S(1)} %get-tuple-element.12), kind=kOutput, calls=%fused_computation.165 | convolution fusion | flops 9688842240 | bytes 28340224 | tf_op jit(solution)/shard_map/dot_general | solution.py:74
  331.0 3.2 reshape.125
  335.2 3.1 slice_reduce_fusion.5
  350.5 27.4 %all-gather.13.cloned.1.call-done = bf16[2048,1536]{1,0:T(8,128)(2,1)} async-done(((bf16[128,1536]{1,0:T(8,128)(2,1)}), bf16[2048,1536]{1,0:T(8,128)(2,1)}) %all-gather.13.cloned.1.call-update) | async-done | bytes 6291472 | tf_op jit(solution)/shard_map/all_gather | solution.py:59
  377.9 4.7 fusion.26
  384.6 55.6 %all-gather.15.cloned.1.call-done = bf16[2048,1536]{1,0:T(8,128)(2,1)} async-done(((bf16[128,1536]{1,0:T(8,128)(2,1)}), bf16[2048,1536]{1,0:T(8,128)(2,1)}) %all-gather.15.cloned.1.call-update) | async-done | bytes 6291472 | tf_op jit(solution)/shard_map/all_gather | solution.py:59
  440.2 4.7 fusion.32
  446.4 56.1 %all-gather.17.cloned.1.call-done = bf16[2048,1536]{1,0:T(8,128)(2,1)} async-done(((bf16[128,1536]{1,0:T(8,128)(2,1)}), bf16[2048,1536]{1,0:T(8,128)(2,1)}) %all-gather.17.cloned.1.call-update) | async-done | bytes 6291472 | tf_op jit(solution)/shard_map/all_gather | solution.py:59
  502.5 3.9 fusion.38
  507.9 3.7 add_convert_fusion.2
  511.7 3.2 add_convert_fusion.1
  515.0 16.7 %collective-permute-done.3 = bf16[512,1024]{1,0:T(8,128)(2,1)S(1)} collective-permute-done((bf16[512,1024]{1,0:T(8,128)(2,1)S(1)}, bf16[512,1024]{1,0:T(8,128)(2,1)S(1)}, u32[]{:S(2)}, u32[]{:S(2)}) %collective-permute-start.3) | collective-permute-done | bytes 1048608 | tf_op jit(solution)/shard_map/ppermute | solution.py:89
  (137 shorter events, 77.1 us)
Async XLA Ops:
  7.2 126.9 %all-gather.9.cloned.1.call-start = ((), (), s32[]{:S(2)}) async-start(), calls=%async_computation.1 | async-start | bytes 20054016 | tf_op jit(solution)/shard_map/all_gather | solution.py:52
  11.1 202.9 %all-gather.11.cloned.1.call-start = ((), (), s32[]{:S(2)}) async-start(), calls=%async_computation.2 | async-start | bytes 20054016 | tf_op jit(solution)/shard_map/all_gather | solution.py:52
  12.7 301.7 %all-gather.7.cloned.1.call-start = ((), (), s32[]{:S(2)}) async-start(), calls=%async_computation | async-start | bytes 20054016 | tf_op jit(solution)/shard_map/all_gather | solution.py:52
  14.2 8.8 %copy-start.1 = (bf16[384,12,384]{2,0,1:T(8,128)(2,1)S(1)}, bf16[384,12,384]{2,0,1:T(8,128)(2,1)}, u32[]{:S(2)}) copy-start(bf16[384,12,384]{2,0,1:T(8,128)(2,1)} %param.11) | copy-start | bytes 10616836
  14.2 363.7 %all-gather.13.cloned.1.call-start = ((), (), s32[]{:S(2)}) async-start(), calls=%async_computation.3 | async-start | bytes 6684672 | tf_op jit(solution)/shard_map/all_gather | solution.py:59
  16.7 423.5 %all-gather.15.cloned.1.call-start = ((), (), s32[]{:S(2)}) async-start(), calls=%async_computation.4 | async-start | bytes 6684672 | tf_op jit(solution)/shard_map/all_gather | solution.py:59
  17.3 485.1 %all-gather.17.cloned.1.call-start = ((), (), s32[]{:S(2)}) async-start(), calls=%async_computation.5 | async-start | bytes 6684672 | tf_op jit(solution)/shard_map/all_gather | solution.py:59
  17.4 107.6 %collective-permute-start = (bf16[512,3072]{1,0:T(8,128)(2,1)}, bf16[512,3072]{1,0:T(8,128)(2,1)}, u32[]{:S(2)}, u32[]{:S(2)}) collective-permute-start(bf16[512,3072]{1,0:T(8,128)(2,1)} %param.7), channel_id=1, source_target_pairs={{0,1},{1,0},{2,3},{3,2},{4,5},{5,4},{6,7},{7,6},{8,9},{9,8},{10,11... | collective-permute-start | bytes 9437192 | tf_op jit(solution)/shard_map/ppermute | solution.py:64
  128.3 1.7 copy-start
  129.9 4.2 copy-start.12
  242.8 12.4 %copy-start.10 = (f32[128]{0:T(128)S(1)}, f32[128]{0:T(128)}, u32[]{:S(2)}) copy-start(f32[128]{0:T(128)} %param.10) | copy-start | bytes 1540
  242.8 12.5 %copy-start.11 = (f32[128]{0:T(128)S(1)}, f32[128]{0:T(128)}, u32[]{:S(2)}) copy-start(f32[128]{0:T(128)} %param.9) | copy-start | bytes 1540
  338.3 5.4 copy-start.2
  338.3 5.4 copy-start.3
  347.0 2.8 copy-start.8
  350.5 33.5 %copy-start.13 = (f32[2]{0:T(128)S(1)}, f32[2]{0:T(128)}, u32[]{:S(2)}) copy-start(f32[2]{0:T(128)} %constant.46) | copy-start | bytes 28
  382.6 125.3 %collective-permute-start.1 = (bf16[512,1024]{1,0:T(8,128)(2,1)}, bf16[512,1024]{1,0:T(8,128)(2,1)S(1)}, u32[]{:S(2)}, u32[]{:S(2)}) collective-permute-start(bf16[512,1024]{1,0:T(8,128)(2,1)} %fusion.26), channel_id=1, source_target_pairs={{0,1},{1,0},{2,3},{3,2},{4,5},{5,4},{6,7},{7,6},{8,9},{9,8},{10,11... | collective-permute-start | bytes 3145736 | tf_op jit(solution)/shard_map/ppermute | solution.py:89
  444.9 66.7 %collective-permute-start.2 = (bf16[512,1024]{1,0:T(8,128)(2,1)}, bf16[512,1024]{1,0:T(8,128)(2,1)}, u32[]{:S(2)}, u32[]{:S(2)}) collective-permute-start(bf16[512,1024]{1,0:T(8,128)(2,1)} %fusion.32), channel_id=1, source_target_pairs={{0,1},{1,0},{2,3},{3,2},{4,5},{5,4},{6,7},{7,6},{8,9},{9,8},{10,11... | collective-permute-start | bytes 3145736 | tf_op jit(solution)/shard_map/ppermute | solution.py:89
  502.5 9.2 %slice-start = ((s8[6291456]{0:T(1024)(128)(4,1)}), s8[4194304]{0:T(1024)(128)(4,1)S(1)}, s32[]{:S(2)}) async-start(s8[6291456]{0:T(1024)(128)(4,1)} %bitcast.41), calls=%async_computation.6 | async-start | bytes 8388608
  506.3 5.3 slice-start.1
  506.3 25.4 %collective-permute-start.3 = (bf16[512,1024]{1,0:T(8,128)(2,1)S(1)}, bf16[512,1024]{1,0:T(8,128)(2,1)S(1)}, u32[]{:S(2)}, u32[]{:S(2)}) collective-permute-start(bf16[512,1024]{1,0:T(8,128)(2,1)S(1)} %fusion.38), channel_id=1, source_target_pairs={{0,1},{1,0},{2,3},{3,2},{4,5},{5,4},{6,7},{7,6},{8,9},{9,8},{10,11... | collective-permute-start | bytes 3145736 | tf_op jit(solution)/shard_map/ppermute | solution.py:89
  511.6 20.1 %slice-start.2 = ((s8[6291456]{0:T(1024)(128)(4,1)}), s8[4194304]{0:T(1024)(128)(4,1)S(1)}, s32[]{:S(2)}) async-start(s8[6291456]{0:T(1024)(128)(4,1)} %bitcast.43), calls=%async_computation.8 | async-start | bytes 8388608
  511.6 20.1 %slice-start.3 = ((s8[6291456]{0:T(1024)(128)(4,1)}), s8[2097152]{0:T(1024)(128)(4,1)S(1)}, s32[]{:S(2)}) async-start(s8[6291456]{0:T(1024)(128)(4,1)} %bitcast.43), calls=%async_computation.9 | async-start | bytes 4194304
  534.8 1.7 copy-start.9
  (4 other events, 5.0 us)
Sparse Core Ops, SparseCore 0:
  11.2 102.4 all-gather.8
  115.3 98.7 all-gather.10
  215.6 98.7 all-gather.6
  316.5 61.3 all-gather.12
  380.0 60.0 all-gather.14
  442.3 60.0 all-gather.16
where the time goes:
time: 548 us; the launch traced here: 544 us
  waiting for transfers between devices  246 us (45%)
  blocking collectives  98.2 us (18%)
  matrix products  89.1 us (16%)
  local copies, waits for them, and re-layouts  50.6 us (9%)
  other arithmetic  36.9 us (7%)
  between operations  14.9 us (3%)
  starting transfers between devices  7.74 us (1%)
    all_gather x3, waiting for transfers between devices, shards(): out_pieces.append(lax.all_gather(part, 'rep', axis=0, tiled=True))  139 us
    psum x1, blocking collectives, shards(): totals = lax.psum(jnp.stack([local_in, local_out]), ('rep', 'tp'))  98.2 us
    all_gather x3, waiting for transfers between devices, shards(): pieces.append(lax.all_gather(part, 'rep', axis=0, tiled=True))  89.7 us
    dot_general x3, matrix products, shards(): projected = jnp.dot(normed, piece, preferred_element_type=jnp.float32)  50.8 us
    unnamed x73, local copies, waits for them, and re-layouts  22.8 us
    dot_general x6, matrix products, product(): lax.dot_general(mixed, rows, (((1,), (1,)), ((), ())), preferred_element_...  22 us
    ppermute x3, waiting for transfers between devices, shards(): arrived = lax.ppermute(sent, 'tp', swap)  16.8 us
    reduce_sum x6, other arithmetic, layer_norm(): variance = jnp.mean(centred * centred, -1, keepdims=True)  14.3 us
  transfers between devices with their start and end apart: 10, of which 6 were waited for; matrix products, arithmetic and copies ran while one was open for 30% of the time, Pallas kernels for 0%

commit v1 on v0

--- a/solution.py
+++ b/solution.py
@@ -59,7 +59,7 @@
         out_pieces.append(lax.all_gather(part, "rep", axis=0, tiled=True))
     local_in = jnp.sum(jnp.square(project_in.astype(jnp.float32)))
     local_out = jnp.sum(jnp.square(project_out.astype(jnp.float32)))
-    totals = lax.psum(jnp.stack([local_in, local_out]), ("rep", "tp"))
+    totals = lax.psum(lax.psum(jnp.stack([local_in, local_out]), "tp"), "rep")
     if n_tp == 2:
         other = lax.ppermute(activations, "tp", swap)
         other, totals = lax.optimization_barrier((other, totals))

time: 548 us -> 553 us (level)
    psum x1 -> x2, blocking collectives: 98.2 us -> 95.9 us  [shards(): totals = lax.psum(lax.psum(jnp.stack([local_in, local_out]), 'tp'), 'rep')]
where the time goes in v1:
time: 553 us; the launch traced here: 543 us
  waiting for transfers between devices  248 us (45%)
  blocking collectives  95.9 us (17%)
  matrix products  89.1 us (16%)
  local copies, waits for them, and re-layouts  50.6 us (9%)
  other arithmetic  36.9 us (7%)
  between operations  14.9 us (3%)
  starting transfers between devices  7.75 us (1%)
    all_gather x3, waiting for transfers between devices, shards(): out_pieces.append(lax.all_gather(part, 'rep', axis=0, tiled=True))  139 us
    psum x2, blocking collectives, shards(): totals = lax.psum(lax.psum(jnp.stack([local_in, local_out]), 'tp'), 'rep')  95.9 us
    all_gather x3, waiting for transfers between devices, shards(): pieces.append(lax.all_gather(part, 'rep', axis=0, tiled=True))  91.6 us
    dot_general x3, matrix products, shards(): projected = jnp.dot(normed, piece, preferred_element_type=jnp.float32)  50.8 us
    unnamed x73, local copies, waits for them, and re-layouts  22.7 us
    dot_general x6, matrix products, product(): lax.dot_general(mixed, rows, (((1,), (1,)), ((), ())), preferred_element_...  22 us
    ppermute x3, waiting for transfers between devices, shards(): arrived = lax.ppermute(sent, 'tp', swap)  16.8 us
    reduce_sum x6, other arithmetic, layer_norm(): variance = jnp.mean(centred * centred, -1, keepdims=True)  14.3 us
  transfers between devices with their start and end apart: 10, of which 6 were waited for; matrix products, arithmetic and copies ran while one was open for 30% of the time, Pallas kernels for 0%

profile of v1, /device:TPU:0, one launch (start us, length us, event | category | flops | bytes accessed | tf_op | source)
XLA Modules:
  0.0 543.2 jit_solution(18231373607069116772)
XLA Ops:
  26.8 62.1 %psum.14 = f32[2]{0:T(128)S(1)} all-reduce(f32[2]{0:T(128)S(1)} %pad_maximum_fusion.1), channel_id=1, replica_groups=mesh['rep'=16,'tp'=2] {'tp'}, use_global_device_ids=true, to_apply=%region_2.0 | all-reduce | flops 2 | bytes 16 | tf_op jit(solution)/shard_map/psum | solution.py:62
  88.9 33.8 %psum.15 = f32[2]{0:T(128)S(1)} all-reduce(f32[2]{0:T(128)S(1)} %psum.14), channel_id=1, replica_groups=mesh['rep'=16,'tp'=2] {'rep'}, use_global_device_ids=true, to_apply=%region_3.0 | all-reduce | flops 2 | bytes 16 | tf_op jit(solution)/shard_map/psum | solution.py:62
  122.7 3.3 broadcast_select_fusion.1
  127.6 4.1 fusion.5
  131.8 17.0 %fusion.109 = f32[512,1536]{1,0:T(8,128)} fusion(bf16[6144,1536]{0,1:T(8,128)(2,1)} %all-gather.9.cloned.1.call-done, f32[6144]{0:T(1024)S(1)} %copy-done.12, f32[512]{0:T(512)S(1)} %add_rsqrt_fusion.6, f32[512]{0:T(512)S(1)} %broadcast_multiply_fusion.6, bf16[512,3072]{1,0:T(8,128)(2,1)} %copy-done, bf16[512,3072]{1,0:T(8,128)(2,1)S(1)} %get-tuple-element.12), kind=kOutput, calls=%fused_computation.164 | convolution fusion | flops 9688842240 | bytes 28340224 | tf_op jit(solution)/shard_map/dot_general | solution.py:74
  148.8 4.8 reshape.128
  153.6 60.0 %all-gather.11.cloned.1.call-done = bf16[6144,1536]{0,1:T(8,128)(2,1)} async-done(((bf16[384,1536]{0,1:T(8,128)(2,1)}), bf16[6144,1536]{0,1:T(8,128)(2,1)}) %all-gather.11.cloned.1.call-update) | async-done | bytes 18874384 | tf_op jit(solution)/shard_map/all_gather | solution.py:52
  213.6 17.2 %fusion.107 = f32[512,1536]{1,0:T(8,128)} fusion(bf16[6144,1536]{0,1:T(8,128)(2,1)} %all-gather.11.cloned.1.call-done, f32[6144]{0:T(1024)S(1)} %copy-done.12, f32[512]{0:T(512)S(1)} %add_rsqrt_fusion.6, f32[512]{0:T(512)S(1)} %broadcast_multiply_fusion.6, bf16[512,3072]{1,0:T(8,128)(2,1)} %copy-done, bf16[512,3072]{1,0:T(8,128)(2,1)S(1)} %get-tuple-element.12), kind=kOutput, calls=%fused_computation.163 | convolution fusion | flops 9688842240 | bytes 28340224 | tf_op jit(solution)/shard_map/dot_general | solution.py:74
  230.8 4.9 reshape.131
  235.7 6.6 %slice_reduce_fusion.1 = (f32[2,256,4]{2,1,0:T(8,128)}, f32[2,256,4]{2,1,0:T(8,128)}, f32[2,256,4,128]{3,2,1,0:T(4,128)}, f32[2,256,4,128]{3,2,1,0:T(4,128)}, f3...) fusion(f32[2,256,4,384]{3,2,1,0:T(4,128)} %reshape.131, ...), kind=kLoop, calls=%fused_computation.158 | loop fusion | flops 1040384 | bytes 8421376 | tf_op jit(solution)/shard_map/reduce_sum | solution.py:15
  259.6 3.5 fusion.49
  276.8 3.4 fusion.48
  282.3 31.6 %all-gather.7.cloned.1.call-done = bf16[6144,1536]{0,1:T(8,128)(2,1)} async-done(((bf16[384,1536]{0,1:T(8,128)(2,1)}), bf16[6144,1536]{0,1:T(8,128)(2,1)}) %all-gather.7.cloned.1.call-update) | async-done | bytes 18874384 | tf_op jit(solution)/shard_map/all_gather | solution.py:52
  313.9 16.6 %fusion.111 = f32[512,1536]{1,0:T(8,128)} fusion(bf16[6144,1536]{0,1:T(8,128)(2,1)} %all-gather.7.cloned.1.call-done, f32[6144]{0:T(1024)S(1)} %copy-done.12, f32[512]{0:T(512)S(1)} %add_rsqrt_fusion.6, f32[512]{0:T(512)S(1)} %broadcast_multiply_fusion.6, bf16[512,3072]{1,0:T(8,128)(2,1)} %copy-done, bf16[512,3072]{1,0:T(8,128)(2,1)S(1)} %get-tuple-element.12), kind=kOutput, calls=%fused_computation.165 | convolution fusion | flops 9688842240 | bytes 28340224 | tf_op jit(solution)/shard_map/dot_general | solution.py:74
  330.6 3.2 reshape.125
  350.1 27.4 %all-gather.13.cloned.1.call-done = bf16[2048,1536]{1,0:T(8,128)(2,1)} async-done(((bf16[128,1536]{1,0:T(8,128)(2,1)}), bf16[2048,1536]{1,0:T(8,128)(2,1)}) %all-gather.13.cloned.1.call-update) | async-done | bytes 6291472 | tf_op jit(solution)/shard_map/all_gather | solution.py:59
  377.5 4.7 fusion.26
  384.2 55.6 %all-gather.15.cloned.1.call-done = bf16[2048,1536]{1,0:T(8,128)(2,1)} async-done(((bf16[128,1536]{1,0:T(8,128)(2,1)}), bf16[2048,1536]{1,0:T(8,128)(2,1)}) %all-gather.15.cloned.1.call-update) | async-done | bytes 6291472 | tf_op jit(solution)/shard_map/all_gather | solution.py:59
  439.8 4.7 fusion.32
  446.0 56.1 %all-gather.17.cloned.1.call-done = bf16[2048,1536]{1,0:T(8,128)(2,1)} async-done(((bf16[128,1536]{1,0:T(8,128)(2,1)}), bf16[2048,1536]{1,0:T(8,128)(2,1)}) %all-gather.17.cloned.1.call-update) | async-done | bytes 6291472 | tf_op jit(solution)/shard_map/all_gather | solution.py:59
  502.0 3.9 fusion.38
  507.4 3.7 add_convert_fusion.2
  511.3 3.2 add_convert_fusion.1
  514.5 16.7 %collective-permute-done.3 = bf16[512,1024]{1,0:T(8,128)(2,1)S(1)} collective-permute-done((bf16[512,1024]{1,0:T(8,128)(2,1)S(1)}, bf16[512,1024]{1,0:T(8,128)(2,1)S(1)}, u32[]{:S(2)}, u32[]{:S(2)}) %collective-permute-start.3) | collective-permute-done | bytes 1048608 | tf_op jit(solution)/shard_map/ppermute | solution.py:89
  (138 shorter events, 80.2 us)
Async XLA Ops:
  7.2 124.6 %all-gather.9.cloned.1.call-start = ((), (), s32[]{:S(2)}) async-start(), calls=%async_computation.1 | async-start | bytes 20054016 | tf_op jit(solution)/shard_map/all_gather | solution.py:52
  11.1 202.5 %all-gather.11.cloned.1.call-start = ((), (), s32[]{:S(2)}) async-start(), calls=%async_computation.2 | async-start | bytes 20054016 | tf_op jit(solution)/shard_map/all_gather | solution.py:52
  12.7 301.3 %all-gather.7.cloned.1.call-start = ((), (), s32[]{:S(2)}) async-start(), calls=%async_computation | async-start | bytes 20054016 | tf_op jit(solution)/shard_map/all_gather | solution.py:52
  14.2 8.8 %copy-start.1 = (bf16[384,12,384]{2,0,1:T(8,128)(2,1)S(1)}, bf16[384,12,384]{2,0,1:T(8,128)(2,1)}, u32[]{:S(2)}) copy-start(bf16[384,12,384]{2,0,1:T(8,128)(2,1)} %param.11) | copy-start | bytes 10616836
  14.2 363.3 %all-gather.13.cloned.1.call-start = ((), (), s32[]{:S(2)}) async-start(), calls=%async_computation.3 | async-start | bytes 6684672 | tf_op jit(solution)/shard_map/all_gather | solution.py:59
  16.7 423.0 %all-gather.15.cloned.1.call-start = ((), (), s32[]{:S(2)}) async-start(), calls=%async_computation.4 | async-start | bytes 6684672 | tf_op jit(solution)/shard_map/all_gather | solution.py:59
  17.3 484.7 %all-gather.17.cloned.1.call-start = ((), (), s32[]{:S(2)}) async-start(), calls=%async_computation.5 | async-start | bytes 6684672 | tf_op jit(solution)/shard_map/all_gather | solution.py:59
  17.4 105.3 %collective-permute-start = (bf16[512,3072]{1,0:T(8,128)(2,1)}, bf16[512,3072]{1,0:T(8,128)(2,1)}, u32[]{:S(2)}, u32[]{:S(2)}) collective-permute-start(bf16[512,3072]{1,0:T(8,128)(2,1)} %param.7), channel_id=1, source_target_pairs={{0,1},{1,0},{2,3},{3,2},{4,5},{5,4},{6,7},{7,6},{8,9},{9,8},{10,11... | collective-permute-start | bytes 9437192 | tf_op jit(solution)/shard_map/ppermute | solution.py:64
  125.9 1.7 copy-start
  127.6 4.2 copy-start.12
  242.3 12.4 %copy-start.10 = (f32[128]{0:T(128)S(1)}, f32[128]{0:T(128)}, u32[]{:S(2)}) copy-start(f32[128]{0:T(128)} %param.10) | copy-start | bytes 1540
  242.3 12.5 %copy-start.11 = (f32[128]{0:T(128)S(1)}, f32[128]{0:T(128)}, u32[]{:S(2)}) copy-start(f32[128]{0:T(128)} %param.9) | copy-start | bytes 1540
  337.9 5.4 copy-start.2
  337.9 5.4 copy-start.3
  346.5 2.8 copy-start.8
  350.1 33.6 %copy-start.13 = (f32[2]{0:T(128)S(1)}, f32[2]{0:T(128)}, u32[]{:S(2)}) copy-start(f32[2]{0:T(128)} %constant.46) | copy-start | bytes 28
  382.2 125.3 %collective-permute-start.1 = (bf16[512,1024]{1,0:T(8,128)(2,1)}, bf16[512,1024]{1,0:T(8,128)(2,1)S(1)}, u32[]{:S(2)}, u32[]{:S(2)}) collective-permute-start(bf16[512,1024]{1,0:T(8,128)(2,1)} %fusion.26), channel_id=1, source_target_pairs={{0,1},{1,0},{2,3},{3,2},{4,5},{5,4},{6,7},{7,6},{8,9},{9,8},{10,11... | collective-permute-start | bytes 3145736 | tf_op jit(solution)/shard_map/ppermute | solution.py:89
  444.5 66.7 %collective-permute-start.2 = (bf16[512,1024]{1,0:T(8,128)(2,1)}, bf16[512,1024]{1,0:T(8,128)(2,1)}, u32[]{:S(2)}, u32[]{:S(2)}) collective-permute-start(bf16[512,1024]{1,0:T(8,128)(2,1)} %fusion.32), channel_id=1, source_target_pairs={{0,1},{1,0},{2,3},{3,2},{4,5},{5,4},{6,7},{7,6},{8,9},{9,8},{10,11... | collective-permute-start | bytes 3145736 | tf_op jit(solution)/shard_map/ppermute | solution.py:89
  502.0 9.2 %slice-start = ((s8[6291456]{0:T(1024)(128)(4,1)}), s8[4194304]{0:T(1024)(128)(4,1)S(1)}, s32[]{:S(2)}) async-start(s8[6291456]{0:T(1024)(128)(4,1)} %bitcast.41), calls=%async_computation.6 | async-start | bytes 8388608
  505.9 5.3 slice-start.1
  505.9 25.4 %collective-permute-start.3 = (bf16[512,1024]{1,0:T(8,128)(2,1)S(1)}, bf16[512,1024]{1,0:T(8,128)(2,1)S(1)}, u32[]{:S(2)}, u32[]{:S(2)}) collective-permute-start(bf16[512,1024]{1,0:T(8,128)(2,1)S(1)} %fusion.38), channel_id=1, source_target_pairs={{0,1},{1,0},{2,3},{3,2},{4,5},{5,4},{6,7},{7,6},{8,9},{9,8},{10,11... | collective-permute-start | bytes 3145736 | tf_op jit(solution)/shard_map/ppermute | solution.py:89
  511.2 20.1 %slice-start.2 = ((s8[6291456]{0:T(1024)(128)(4,1)}), s8[4194304]{0:T(1024)(128)(4,1)S(1)}, s32[]{:S(2)}) async-start(s8[6291456]{0:T(1024)(128)(4,1)} %bitcast.43), calls=%async_computation.8 | async-start | bytes 8388608
  511.2 20.1 %slice-start.3 = ((s8[6291456]{0:T(1024)(128)(4,1)}), s8[2097152]{0:T(1024)(128)(4,1)S(1)}, s32[]{:S(2)}) async-start(s8[6291456]{0:T(1024)(128)(4,1)} %bitcast.43), calls=%async_computation.9 | async-start | bytes 4194304
  534.4 1.7 copy-start.9
  (4 other events, 5.0 us)
Sparse Core Ops, SparseCore 0:
  11.2 101.7 all-gather.8
  114.6 98.9 all-gather.10
  215.2 98.7 all-gather.6
  316.1 61.3 all-gather.12
  379.6 60.0 all-gather.14
  441.9 60.0 all-gather.16
